TPU v7x, 32 devices: a whole 2x2x4 slice. The times are simulated.
32 devices in a mesh: hi: 4 (over y, core), lo: 8 (over z, x).
Axes of the slice: x: 2, y: 2, z: 4, core: 2. Of those that a mesh axis runs over, the one named last changes fastest.
Arguments:
- grm: bfloat16 [4, 8, 64, 4, 512], P(None, 'lo', None, 'hi'), as said below
- right_sides: float32 [2048, 512], P(('hi', 'lo')), may hold values from -6 to 6
- inv_diag: float32 [2048], P(('hi', 'lo')), may hold values from 0.3 to 1
- bases: float32 [2048, 576], P(('hi', 'lo')), may hold values from -0.75 to 0.75
- couplings: float32 [9, 64, 64], replicated, as said below
- level_map: int32 [8], replicated, may hold values from 0 to 7, each once
- variance: float32 [2], replicated, may hold values from 0.3 to 1.5
- iters_per_column: int32 [512], replicated, may hold values from 1 to 3
Outputs:
- solution: float32 [2048, 512], P(('hi', 'lo'))
- residual: float32 [2048, 512], P(('hi', 'lo'))
Inputs may be any that keep to these rules, and one draw needn't show every extreme that they name: `grm`: G is symmetric and positive definite. `couplings`: each of the 9 matrices is symmetric and positive definite. `level_map`: a permutation of the levels.
All inputs are finite; a program needn't handle non-finite values.
Results may differ from a plain program's by a relative error of at most 0.0055.
Values may be sent and summed in bfloat16 or wider, within the bound.
A program may use at most 64 MiB of HBM per device.

v0:
```python
import jax
import jax.numpy as jnp
from jax import lax
from jax.sharding import PartitionSpec as P

ITERS = 3


def from_partner(value, axis, bit):
    mask = 2**bit
    pairs = [(source, source ^ mask) for source in range(lax.axis_size(axis))]
    return lax.ppermute(value, axis, pairs)


def level_pieces(coefficients, couplings, level):
    level_ids = jnp.arange(couplings.shape[0], dtype=jnp.int32)
    select = (level_ids == level).astype(jnp.float32)
    own_part = jnp.einsum("l,lrb->rb", select, coefficients)
    matrix = jnp.einsum("l,lrs->rs", select, couplings)
    return (own_part, matrix, select)


def add_level(stacked, own_part, other_part, matrix, select):
    term = jnp.dot(matrix, own_part + other_part, precision=lax.Precision.HIGHEST)
    return stacked + select[:, None, None] * term[None]


def local(grm, right_sides, inv_diag, bases, couplings, level_map, variance, iters_per_column):
    row_count, column_count = right_sides.shape
    grm_block = grm.reshape(-1, grm.shape[4])
    level_total = couplings.shape[0]
    rank_width = couplings.shape[1]
    lo_bits = lax.axis_size("lo").bit_length() - 1
    hi_bits = lax.axis_size("hi").bit_length() - 1
    genetic = variance[0]
    noise = variance[1]

    def precondition(resid):
        coefficients = lax.dot_general(
            bases, resid, (((0,), (0,)), ((), ())), precision=lax.Precision.HIGHEST
        )
        coefficients = coefficients.reshape(level_total, rank_width, column_count)
        stacked = jnp.zeros((level_total - 1, rank_width, column_count), jnp.float32)
        for bit_index in range(lo_bits):
            own_part, matrix, select = level_pieces(coefficients, couplings, level_map[bit_index])
            other_part = from_partner(own_part.astype(jnp.bfloat16), "lo", bit_index).astype(
                own_part.dtype
            )
            stacked = add_level(stacked, own_part, other_part, matrix, select[: level_total - 1])
        for bit_index in range(hi_bits):
            own_part, matrix, select = level_pieces(
                coefficients, couplings, level_map[lo_bits + bit_index]
            )
            other_part = from_partner(own_part.astype(jnp.bfloat16), "hi", bit_index).astype(
                own_part.dtype
            )
            stacked = add_level(stacked, own_part, other_part, matrix, select[: level_total - 1])
        split_at = (level_total - 1) * rank_width
        local_part = inv_diag[:, None] * resid + jnp.dot(
            bases[:, :split_at],
            stacked.reshape(split_at, column_count),
            precision=lax.Precision.HIGHEST,
        )
        coarse_basis = bases[:, split_at:]
        partial_energy = jnp.sum(resid * local_part, axis=0)
        total, summed_energy = lax.psum(
            (coefficients[level_total - 1], partial_energy), ("hi", "lo")
        )
        coarse = jnp.dot(couplings[level_total - 1], total, precision=lax.Precision.HIGHEST)
        scaled = local_part + jnp.dot(coarse_basis, coarse, precision=lax.Precision.HIGHEST)
        energy = summed_energy + jnp.sum(total * coarse, axis=0)
        return (scaled, energy)

    solution = jnp.zeros_like(right_sides)
    residual = right_sides
    scaled, energy = precondition(residual)
    direction = scaled
    for step in range(ITERS):
        rounded = direction.astype(jnp.bfloat16)
        partial_value = jnp.dot(
            grm_block,
            lax.all_gather(rounded, "lo", axis=0, tiled=True),
            preferred_element_type=jnp.float32,
        )
        product = lax.psum_scatter(partial_value, "hi", scatter_dimension=0, tiled=True)
        image = genetic * product + noise * direction
        curvature = lax.psum(jnp.sum(direction * image, axis=0), ("hi", "lo"))
        alpha = energy / curvature
        stepsize = jnp.where(step < iters_per_column, alpha, jnp.zeros_like(alpha))
        solution = solution + stepsize * direction
        residual = residual - stepsize * image
        if step + 1 < ITERS:
            scaled, fresh = precondition(residual)
            direction = scaled + fresh / energy * direction
            energy = fresh
    return (solution, residual)


def solution(mesh):
    in_specs = (
        P(None, "lo", None, "hi", None),
        P(("hi", "lo"), None),
        P(("hi", "lo")),
        P(("hi", "lo"), None),
        P(),
        P(),
        P(),
        P(),
    )
    out_specs = (P(("hi", "lo"), None), P(("hi", "lo"), None))
    return jax.shard_map(local, mesh=mesh, in_specs=in_specs, out_specs=out_specs, check_vma=False)
```

profile of v0, /device:TPU:0, one launch (start us, length us, event | category | flops | bytes accessed | tf_op | source)
XLA Modules:
  0.0 806.3 jit_solution(18174941709177877963)
XLA Ops:
  7.2 1.5 fusion.146
  8.7 2.1 fusion.150
  12.1 3.1 collective-permute-start.1
  15.3 1.4 fusion.24
  16.6 2.7 collective-permute-start.2
  19.3 1.4 fusion.22
  20.8 1.4 fusion.20
  22.1 1.6 collective-permute-start.4
  23.7 1.4 fusion.28
  25.1 1.6 collective-permute-start
  35.8 112.5 %all-reduce.5.cloned.1.call-done = f32[64,512]{1,0:T(8,128)} async-done(((f32[64,512]{1,0:T(8,128)}), f32[64,512]{1,0:T(8,128)}) %all-reduce.5.cloned.1.call-update) | async-done | bytes 131088 | tf_op jit(solution)/shard_map/psum | solution.py:66
  152.7 31.3 %all_gather.9 = bf16[512,512]{1,0:T(8,128)(2,1)S(1)} all-gather(bf16[64,512]{1,0:T(8,128)(2,1)S(1)} %get-tuple-element.19), channel_id=1, replica_groups=mesh['hi'=4,'lo'=8] {'lo'}, dimensions={0}, use_global_device_ids=true | all-gather | bytes 589824 | tf_op jit(solution)/shard_map/all_gather | solution.py:82
  185.8 20.3 %reduce-scatter.4.cloned.1.call-done = f32[64,512]{1,0:T(8,128)} async-done(((f32[256,512]{1,0:T(8,128)}), f32[64,512]{1,0:T(8,128)}) %reduce-scatter.4.cloned.1.call-update) | async-done | bytes 131088 | tf_op jit(solution)/shard_map/reduce_scatter | solution.py:85
  206.1 2.2 multiply_reduce_fusion.4
  208.3 39.5 %all-reduce = (f32[512]{0:T(512)S(1)}, f32[512]{0:T(512)S(1)}) all-reduce(f32[512]{0:T(512)S(1)} %get-tuple-element.21, f32[512]{0:T(512)S(1)} %multiply_reduce_fusion.4), channel_id=1, replica_groups=mesh['hi'=4,'lo'=8] {'hi','lo'}, use_global_device_ids=true, to_apply=%region_1.0 | all-reduce | flops 1024 | bytes 8192 | tf_op jit(solution)/shard_map/psum | solution.py:66
  247.8 2.2 multiply_subtract_fusion.2
  251.1 1.3 fusion.16
  252.4 1.4 fusion.14
  253.8 1.4 fusion.12
  255.1 1.4 fusion.10
  257.2 1.4 fusion.18
  258.6 1.5 collective-permute-start.6
  260.2 1.4 collective-permute-start.7
  261.7 2.3 collective-permute-start.9
  264.1 1.6 collective-permute-start.5
  265.6 117.0 %all-reduce.7.cloned.1.call-done = f32[64,512]{1,0:T(8,128)} async-done(((f32[64,512]{1,0:T(8,128)}), f32[64,512]{1,0:T(8,128)}) %all-reduce.7.cloned.1.call-update) | async-done | bytes 131088 | tf_op jit(solution)/shard_map/psum | solution.py:66
  386.6 39.3 %psum.66 = f32[512]{0:T(512)S(1)} all-reduce(f32[512]{0:T(512)S(1)} %get-tuple-element.25), channel_id=1, replica_groups=mesh['hi'=4,'lo'=8] {'hi','lo'}, use_global_device_ids=true, to_apply=%region_8.9 | all-reduce | flops 512 | bytes 4096 | tf_op jit(solution)/shard_map/psum | solution.py:66
  426.1 31.2 %all_gather.10 = bf16[512,512]{1,0:T(8,128)(2,1)S(1)} all-gather(bf16[64,512]{1,0:T(8,128)(2,1)S(1)} %get-tuple-element.29), channel_id=1, replica_groups=mesh['hi'=4,'lo'=8] {'lo'}, dimensions={0}, use_global_device_ids=true | all-gather | bytes 589824 | tf_op jit(solution)/shard_map/all_gather | solution.py:82
  458.5 22.0 %reduce-scatter.6.cloned.1.call-done = f32[64,512]{1,0:T(8,128)} async-done(((f32[256,512]{1,0:T(8,128)}), f32[64,512]{1,0:T(8,128)}) %reduce-scatter.6.cloned.1.call-update) | async-done | bytes 131088 | tf_op jit(solution)/shard_map/reduce_scatter | solution.py:85
  480.5 2.2 multiply_reduce_fusion.2
  482.7 39.5 %psum.68 = f32[512]{0:T(512)S(1)} all-reduce(f32[512]{0:T(512)S(1)} %multiply_reduce_fusion.2), channel_id=1, replica_groups=mesh['hi'=4,'lo'=8] {'hi','lo'}, use_global_device_ids=true, to_apply=%region_13.14 | all-reduce | flops 512 | bytes 4096 | tf_op jit(solution)/shard_map/psum | solution.py:87
  522.2 2.2 multiply_subtract_fusion.1
  525.6 1.3 fusion.6
  526.9 1.4 fusion.4
  528.2 1.4 fusion.2
  529.6 1.4 fusion
  531.7 1.4 fusion.8
  533.1 1.5 collective-permute-start.11
  534.7 1.4 collective-permute-start.12
  536.2 2.3 collective-permute-start.14
  538.5 1.5 collective-permute-start.10
  540.1 117.0 %all-reduce.9.cloned.1.call-done = f32[64,512]{1,0:T(8,128)} async-done(((f32[64,512]{1,0:T(8,128)}), f32[64,512]{1,0:T(8,128)}) %all-reduce.9.cloned.1.call-update) | async-done | bytes 131088 | tf_op jit(solution)/shard_map/psum | solution.py:66
  661.0 39.3 %psum.69 = f32[512]{0:T(512)S(1)} all-reduce(f32[512]{0:T(512)S(1)} %get-tuple-element.31), channel_id=1, replica_groups=mesh['hi'=4,'lo'=8] {'hi','lo'}, use_global_device_ids=true, to_apply=%region_15.16 | all-reduce | flops 512 | bytes 4096 | tf_op jit(solution)/shard_map/psum | solution.py:66
  700.6 31.2 %all_gather.11 = bf16[512,512]{1,0:T(8,128)(2,1)S(1)} all-gather(bf16[64,512]{1,0:T(8,128)(2,1)S(1)} %get-tuple-element.35), channel_id=1, replica_groups=mesh['hi'=4,'lo'=8] {'lo'}, dimensions={0}, use_global_device_ids=true | all-gather | bytes 589824 | tf_op jit(solution)/shard_map/all_gather | solution.py:82
  732.9 22.1 %reduce-scatter.8.cloned.1.call-done = f32[64,512]{1,0:T(8,128)} async-done(((f32[256,512]{1,0:T(8,128)}), f32[64,512]{1,0:T(8,128)}) %reduce-scatter.8.cloned.1.call-update) | async-done | bytes 131088 | tf_op jit(solution)/shard_map/reduce_scatter | solution.py:85
  755.1 2.2 multiply_reduce_fusion
  757.2 39.3 %psum.71 = f32[512]{0:T(512)S(1)} all-reduce(f32[512]{0:T(512)S(1)} %multiply_reduce_fusion), channel_id=1, replica_groups=mesh['hi'=4,'lo'=8] {'hi','lo'}, use_global_device_ids=true, to_apply=%region_20.21 | all-reduce | flops 512 | bytes 4096 | tf_op jit(solution)/shard_map/psum | solution.py:87
  796.6 2.9 multiply_subtract_fusion
  (126 shorter events, 31.0 us)
Async XLA Ops:
  7.2 176.8 %copy-start = (bf16[4,1,64,1,512]{4,2,3,1,0:T(8,128)(2,1)S(1)}, bf16[4,1,64,1,512]{4,2,3,1,0:T(8,128)(2,1)}, u32[]{:S(2)}) copy-start(bf16[4,1,64,1,512]{4,2,3,1,0:T(8,128)(2,1)} %param.8) | copy-start | bytes 786436
  7.2 141.2 %all-reduce.5.cloned.1.call-start = ((), (), s32[]{:S(2)}) async-start(), calls=%async_computation.3 | async-start | bytes 262144 | tf_op jit(solution)/shard_map/psum | solution.py:66
  12.1 137.5 %collective-permute-start.1 = (bf16[64,512]{1,0:T(8,128)(2,1)S(1)}, bf16[64,512]{1,0:T(8,128)(2,1)S(1)}, u32[]{:S(2)}, u32[]{:S(2)}) collective-permute-start(bf16[64,512]{1,0:T(8,128)(2,1)S(1)} %bitcast.372), channel_id=1, source_target_pairs={{0,2},{1,3},{2,0},{3,1},{4,6},{5,7},{6,4},{7,5},{8,10},{9,11},{10,... | collective-permute-start | bytes 196616 | tf_op jit(solution)/shard_map/ppermute | solution.py:12
  16.6 133.3 %collective-permute-start.2 = (bf16[64,512]{1,0:T(8,128)(2,1)S(1)}, bf16[64,512]{1,0:T(8,128)(2,1)S(1)}, u32[]{:S(2)}, u32[]{:S(2)}) collective-permute-start(bf16[64,512]{1,0:T(8,128)(2,1)S(1)} %bitcast.371), channel_id=1, source_target_pairs={{0,4},{1,5},{2,6},{3,7},{4,0},{5,1},{6,2},{7,3},{8,12},{9,13},{10,... | collective-permute-start | bytes 196616 | tf_op jit(solution)/shard_map/ppermute | solution.py:12
  20.7 129.5 %collective-permute-start.3 = (bf16[64,512]{1,0:T(8,128)(2,1)S(1)}, bf16[64,512]{1,0:T(8,128)(2,1)S(1)}, u32[]{:S(2)}, u32[]{:S(2)}) collective-permute-start(bf16[64,512]{1,0:T(8,128)(2,1)S(1)} %bitcast.370), channel_id=1, source_target_pairs={{0,8},{8,0},{16,24},{24,16},{1,9},{9,1},{17,25},{25,17},{2,10},{10... | collective-permute-start | bytes 196616 | tf_op jit(solution)/shard_map/ppermute | solution.py:12
  22.1 8.5 %copy-start.1 = (f32[9,64,64]{2,1,0:T(8,128)S(1)}, f32[9,64,64]{2,1,0:T(8,128)}, u32[]{:S(2)}) copy-start(f32[9,64,64]{2,1,0:T(8,128)} %param.12) | copy-start | bytes 442372
  22.1 128.4 %collective-permute-start.4 = (bf16[64,512]{1,0:T(8,128)(2,1)S(1)}, bf16[64,512]{1,0:T(8,128)(2,1)S(1)}, u32[]{:S(2)}, u32[]{:S(2)}) collective-permute-start(bf16[64,512]{1,0:T(8,128)(2,1)S(1)} %bitcast.368), channel_id=1, source_target_pairs={{0,16},{8,24},{16,0},{24,8},{1,17},{9,25},{17,1},{25,9},{2,18},{10... | collective-permute-start | bytes 196616 | tf_op jit(solution)/shard_map/ppermute | solution.py:12
  25.1 125.7 %collective-permute-start = (bf16[64,512]{1,0:T(8,128)(2,1)S(1)}, bf16[64,512]{1,0:T(8,128)(2,1)S(1)}, u32[]{:S(2)}, u32[]{:S(2)}) collective-permute-start(bf16[64,512]{1,0:T(8,128)(2,1)S(1)} %bitcast.369), channel_id=1, source_target_pairs={{0,1},{1,0},{2,3},{3,2},{4,5},{5,4},{6,7},{7,6},{8,9},{9,8},{10,11... | collective-permute-start | bytes 196616 | tf_op jit(solution)/shard_map/ppermute | solution.py:12
  27.4 178.7 %reduce-scatter.4.cloned.1.call-start = ((), (), s32[]{:S(2)}) async-start(), calls=%async_computation.4 | async-start | bytes 655360 | tf_op jit(solution)/shard_map/reduce_scatter | solution.py:85
  150.5 1.1 copy-start.2
  150.5 1.0 copy-start.3
  150.5 1.0 copy-start.5
  152.7 32.5 %copy-start.6 = (f32[2]{0:T(128)S(1)}, f32[2]{0:T(128)}, u32[]{:S(2)}) copy-start(f32[2]{0:T(128)} %param.14) | copy-start | bytes 28
  184.0 63.8 %copy-start.4 = (s32[512]{0:T(512)S(1)}, s32[512]{0:T(512)}, u32[]{:S(2)}) copy-start(s32[512]{0:T(512)} %param.15) | copy-start | bytes 6148
  185.1 197.5 %all-reduce.7.cloned.1.call-start = ((), (), s32[]{:S(2)}) async-start(), calls=%async_computation.5 | async-start | bytes 262144 | tf_op jit(solution)/shard_map/psum | solution.py:66
  257.2 223.3 %reduce-scatter.6.cloned.1.call-start = ((), (), s32[]{:S(2)}) async-start(), calls=%async_computation.6 | async-start | bytes 655360 | tf_op jit(solution)/shard_map/reduce_scatter | solution.py:85
  258.6 125.2 %collective-permute-start.6 = (bf16[64,512]{1,0:T(8,128)(2,1)S(1)}, bf16[64,512]{1,0:T(8,128)(2,1)S(1)}, u32[]{:S(2)}, u32[]{:S(2)}) collective-permute-start(bf16[64,512]{1,0:T(8,128)(2,1)S(1)} %bitcast.381), channel_id=1, source_target_pairs={{0,2},{1,3},{2,0},{3,1},{4,6},{5,7},{6,4},{7,5},{8,10},{9,11},{10,... | collective-permute-start | bytes 196616 | tf_op jit(solution)/shard_map/ppermute | solution.py:12
  260.2 124.0 %collective-permute-start.7 = (bf16[64,512]{1,0:T(8,128)(2,1)S(1)}, bf16[64,512]{1,0:T(8,128)(2,1)S(1)}, u32[]{:S(2)}, u32[]{:S(2)}) collective-permute-start(bf16[64,512]{1,0:T(8,128)(2,1)S(1)} %bitcast.380), channel_id=1, source_target_pairs={{0,4},{1,5},{2,6},{3,7},{4,0},{5,1},{6,2},{7,3},{8,12},{9,13},{10,... | collective-permute-start | bytes 196616 | tf_op jit(solution)/shard_map/ppermute | solution.py:12
  261.6 122.8 %collective-permute-start.8 = (bf16[64,512]{1,0:T(8,128)(2,1)S(1)}, bf16[64,512]{1,0:T(8,128)(2,1)S(1)}, u32[]{:S(2)}, u32[]{:S(2)}) collective-permute-start(bf16[64,512]{1,0:T(8,128)(2,1)S(1)} %bitcast.378), channel_id=1, source_target_pairs={{0,8},{8,0},{16,24},{24,16},{1,9},{9,1},{17,25},{25,17},{2,10},{10... | collective-permute-start | bytes 196616 | tf_op jit(solution)/shard_map/ppermute | solution.py:12
  261.7 123.0 %collective-permute-start.9 = (bf16[64,512]{1,0:T(8,128)(2,1)S(1)}, bf16[64,512]{1,0:T(8,128)(2,1)S(1)}, u32[]{:S(2)}, u32[]{:S(2)}) collective-permute-start(bf16[64,512]{1,0:T(8,128)(2,1)S(1)} %bitcast.376), channel_id=1, source_target_pairs={{0,16},{8,24},{16,0},{24,8},{1,17},{9,25},{17,1},{25,9},{2,18},{10... | collective-permute-start | bytes 196616 | tf_op jit(solution)/shard_map/ppermute | solution.py:12
  264.1 121.0 %collective-permute-start.5 = (bf16[64,512]{1,0:T(8,128)(2,1)S(1)}, bf16[64,512]{1,0:T(8,128)(2,1)S(1)}, u32[]{:S(2)}, u32[]{:S(2)}) collective-permute-start(bf16[64,512]{1,0:T(8,128)(2,1)S(1)} %bitcast.375), channel_id=1, source_target_pairs={{0,1},{1,0},{2,3},{3,2},{4,5},{5,4},{6,7},{7,6},{8,9},{9,8},{10,11... | collective-permute-start | bytes 196616 | tf_op jit(solution)/shard_map/ppermute | solution.py:12
  458.4 198.6 %all-reduce.9.cloned.1.call-start = ((), (), s32[]{:S(2)}) async-start(), calls=%async_computation.7 | async-start | bytes 262144 | tf_op jit(solution)/shard_map/psum | solution.py:66
  531.7 223.4 %reduce-scatter.8.cloned.1.call-start = ((), (), s32[]{:S(2)}) async-start(), calls=%async_computation.8 | async-start | bytes 655360 | tf_op jit(solution)/shard_map/reduce_scatter | solution.py:85
  533.1 125.2 %collective-permute-start.11 = (bf16[64,512]{1,0:T(8,128)(2,1)S(1)}, bf16[64,512]{1,0:T(8,128)(2,1)S(1)}, u32[]{:S(2)}, u32[]{:S(2)}) collective-permute-start(bf16[64,512]{1,0:T(8,128)(2,1)S(1)} %bitcast.382), channel_id=1, source_target_pairs={{0,2},{1,3},{2,0},{3,1},{4,6},{5,7},{6,4},{7,5},{8,10},{9,11},{10,... | collective-permute-start | bytes 196616 | tf_op jit(solution)/shard_map/ppermute | solution.py:12
  534.7 124.0 %collective-permute-start.12 = (bf16[64,512]{1,0:T(8,128)(2,1)S(1)}, bf16[64,512]{1,0:T(8,128)(2,1)S(1)}, u32[]{:S(2)}, u32[]{:S(2)}) collective-permute-start(bf16[64,512]{1,0:T(8,128)(2,1)S(1)} %bitcast.379), channel_id=1, source_target_pairs={{0,4},{1,5},{2,6},{3,7},{4,0},{5,1},{6,2},{7,3},{8,12},{9,13},{10,... | collective-permute-start | bytes 196616 | tf_op jit(solution)/shard_map/ppermute | solution.py:12
  536.1 122.8 %collective-permute-start.13 = (bf16[64,512]{1,0:T(8,128)(2,1)S(1)}, bf16[64,512]{1,0:T(8,128)(2,1)S(1)}, u32[]{:S(2)}, u32[]{:S(2)}) collective-permute-start(bf16[64,512]{1,0:T(8,128)(2,1)S(1)} %bitcast.377), channel_id=1, source_target_pairs={{0,8},{8,0},{16,24},{24,16},{1,9},{9,1},{17,25},{25,17},{2,10},{10... | collective-permute-start | bytes 196616 | tf_op jit(solution)/shard_map/ppermute | solution.py:12
  536.2 123.0 %collective-permute-start.14 = (bf16[64,512]{1,0:T(8,128)(2,1)S(1)}, bf16[64,512]{1,0:T(8,128)(2,1)S(1)}, u32[]{:S(2)}, u32[]{:S(2)}) collective-permute-start(bf16[64,512]{1,0:T(8,128)(2,1)S(1)} %bitcast.374), channel_id=1, source_target_pairs={{0,16},{8,24},{16,0},{24,8},{1,17},{9,25},{17,1},{25,9},{2,18},{10... | collective-permute-start | bytes 196616 | tf_op jit(solution)/shard_map/ppermute | solution.py:12
  538.5 120.9 %collective-permute-start.10 = (bf16[64,512]{1,0:T(8,128)(2,1)S(1)}, bf16[64,512]{1,0:T(8,128)(2,1)S(1)}, u32[]{:S(2)}, u32[]{:S(2)}) collective-permute-start(bf16[64,512]{1,0:T(8,128)(2,1)S(1)} %bitcast.373), channel_id=1, source_target_pairs={{0,1},{1,0},{2,3},{3,2},{4,5},{5,4},{6,7},{7,6},{8,9},{9,8},{10,11... | collective-permute-start | bytes 196616 | tf_op jit(solution)/shard_map/ppermute | solution.py:12
Sparse Core Ops, SparseCore 0:
  27.5 120.8 all-reduce.4
  185.2 20.8 reduce-scatter.3
  257.3 125.2 all-reduce.6
  458.6 21.9 reduce-scatter.5
  531.8 125.2 all-reduce.8
  733.1 21.9 reduce-scatter.7
where the time goes:
time: 808 us; the launch traced here: 806 us
  waiting for transfers between devices  411 us (51%)
  blocking collectives  291 us (36%)
  matrix products  43.6 us (5%)
  starting transfers between devices  23 us (3%)
  other arithmetic  18.3 us (2%)
  between operations  14.7 us (2%)
    psum x3, waiting for transfers between devices, precondition(): lax.psum((coefficients[level_total - 1], partial_energy), ('hi', 'lo'))  346 us
    psum x3, blocking collectives, precondition(): lax.psum((coefficients[level_total - 1], partial_energy), ('hi', 'lo'))  118 us
    all_gather x3, blocking collectives, local(): lax.all_gather(rounded, 'lo', axis=0, tiled=True)  93.7 us
    psum x2, blocking collectives, local(): curvature = lax.psum(jnp.sum(direction * image, axis=0), ('hi', 'lo'))  78.8 us
    reduce_scatter x3, waiting for transfers between devices, local(): lax.psum_scatter(partial_value, 'hi', scatter_dimension=0, tiled=True)  64.5 us
    ppermute x15, starting transfers between devices, from_partner(): return lax.ppermute(value, axis, pairs)  22.8 us
    dot_general x15, matrix products, level_pieces(): own_part = jnp.einsum('l,lrb->rb', select, coefficients)  20.4 us
  transfers between devices with their start and end apart: 21, of which 6 were waited for; matrix products, arithmetic and copies ran while one was open for 3% of the time, Pallas kernels for 0%

commit v1 on v0

--- a/solution.py
+++ b/solution.py
@@ -1,9 +1,14 @@
+import functools
+
 import jax
 import jax.numpy as jnp
 from jax import lax
+from jax.experimental import pallas as pl
+from jax.experimental.pallas import tpu as pltpu
 from jax.sharding import PartitionSpec as P
 
 ITERS = 3
+MESH = pl.DeviceIdType.MESH
 
 
 def from_partner(value, axis, bit):
@@ -96,6 +101,384 @@
     return (solution, residual)
 
 
+def fits_one_device(mesh, grm, right_sides, bases, couplings):
+    n_hi, n_lo = mesh.shape["hi"], mesh.shape["lo"]
+    devices = n_hi * n_lo
+    samples, columns = right_sides.shape
+    rank = couplings.shape[1]
+    bits = devices.bit_length() - 1
+    used = (bits + 1) * rank
+    width = samples // n_hi
+    return (
+        n_hi == 2 * CORES
+        and n_lo % (2 * XDIM) == 0
+        and columns % (16 * devices) == 0
+        and columns // devices == 16
+        and used % 128 == 0
+        and (bits + 1) % 2 == 0
+        and width % 256 == 0
+        and 2 * rank == 128
+        and 2 * (samples // devices) == 128
+        and samples * (samples + used) * 2 < 2**24
+    )
+
+
+CORES = 2
+XDIM = 2
+
+
+def nt(a, b):
+    return lax.dot_general(a, b, (((1,), (1,)), ((), ())), preferred_element_type=jnp.float32)
+
+
+def nn(a, b):
+    return jnp.dot(a, b, preferred_element_type=jnp.float32)
+
+
+def halves(value, axis):
+    top = value.astype(jnp.bfloat16)
+    rest = (value - top.astype(jnp.float32)).astype(jnp.bfloat16)
+    return jnp.concatenate([top, rest], axis=axis)
+
+
+def whole_kernel(
+    n_hi, n_lo,
+    var_ref, level_ref,
+    grm_ref, rhs_ref, inv_ref, bases_ref, coup_ref, iters_ref,
+    sol_ref, res_ref,
+    pay, xsend, xrecv, isend, irecv, osend, orecv,
+    resid, direct, image, iterate, scaled, inv_row,
+    coef, summed, lifted, couple,
+    send_sem, recv_sem, side_send, side_recv,
+):
+    hi, lo = lax.axis_index("hi"), lax.axis_index("lo")
+    n = n_hi * n_lo
+    me = hi * n_lo + lo
+    y, core = hi // CORES, hi % CORES
+    z, x = lo // XDIM, lo % XDIM
+    depth = n_lo // XDIM
+    rows, columns = rhs_ref.shape
+    mine = columns // n
+    half = mine // 2
+    levels = coup_ref.shape[0]
+    rank = coup_ref.shape[1]
+    bits = n.bit_length() - 1
+    used = (bits + 1) * rank
+    width = grm_ref.shape[2]
+    quad = width // 2
+    samples = rows * n
+    f32, bf16 = jnp.float32, jnp.bfloat16
+
+    barrier = pltpu.get_barrier_semaphore()
+
+    def other(step):
+        peer = lax.rem(me + step, n)
+        return (peer // n_lo, lax.rem(peer, n_lo))
+
+    def greet(step, carry):
+        pl.semaphore_signal(barrier, inc=1, device_id=other(step), device_id_type=MESH)
+        return carry
+
+    lax.fori_loop(1, n, greet, 0)
+
+    column_id = lax.broadcasted_iota(jnp.int32, (1, used), 1)
+    wanted = jnp.full((1, used), (levels - 1) * rank, jnp.int32)
+    for bit in range(bits):
+        wanted = jnp.where(column_id // rank == bit, level_ref[bit] * rank, wanted)
+    wanted = wanted + column_id % rank
+    pick = lax.broadcasted_iota(jnp.int32, (levels * rank, used), 0) == wanted
+    own_bases = nn(bases_ref[...].astype(bf16), pick.astype(f32).astype(bf16))
+    lanes = (
+        slice(0, used + quad),
+        slice(used + quad, used + quad + width),
+        slice(used + quad + width, used + quad + 2 * width),
+    )
+    pay[me, :, 0:used] = own_bases.astype(bf16)
+    across = lax.rem(hi + CORES, n_hi)
+    upper = jnp.where(hi < CORES, lo >= n_lo // 2, lo < n_lo // 2)
+    both = grm_ref[across]
+    pay[me, :, used : used + quad] = jnp.where(
+        upper, both[:, quad:].astype(f32), both[:, :quad].astype(f32)
+    ).astype(bf16)
+    pay[me, :, lanes[1]] = grm_ref[hi]
+    pay[me, :, lanes[2]] = grm_ref[lax.rem(hi + 1, n_hi)]
+
+    turned = rhs_ref[...].T.reshape(n, mine, rows)
+    xsend[...] = jnp.concatenate([turned[:, :half], turned[:, half:]], axis=2)
+    isend[0, :, 0:rows] = inv_ref[...]
+    isend[0, :, rows:] = inv_ref[...]
+
+    couple[...] = jnp.zeros_like(couple)
+    for bit in range(bits + 1):
+        block = coup_ref[level_ref[bit]] if bit < bits else coup_ref[levels - 1]
+        at = slice(bit * rank, (bit + 1) * rank)
+        couple[0, at, at] = block.astype(bf16)
+        couple[1, at, at] = (block - block.astype(bf16).astype(f32)).astype(bf16)
+    taken = lax.broadcasted_iota(jnp.int32, (mine, columns), 1) == (
+        me * mine + lax.broadcasted_iota(jnp.int32, (mine, columns), 0)
+    )
+    steps_wanted = jnp.sum(
+        jnp.where(taken, iters_ref[...].astype(f32), 0.0), axis=1, keepdims=True
+    )
+
+    pl.semaphore_wait(barrier, n - 1)
+
+    def exchange(source, target, kind):
+        def send(step, carry):
+            peer = lax.rem(me + step, n)
+            pltpu.make_async_remote_copy(
+                src_ref=source.at[peer], dst_ref=target.at[me],
+                send_sem=side_send.at[kind], recv_sem=side_recv.at[kind],
+                device_id=(peer // n_lo, lax.rem(peer, n_lo)), device_id_type=MESH,
+            ).start()
+            return carry
+
+        lax.fori_loop(1, n, send, 0)
+        target[me] = source[me]
+
+    def settle(target, kind):
+        all_but_one = target.at[pl.ds(0, n - 1)]
+        pltpu.make_async_copy(all_but_one, all_but_one, side_recv.at[kind]).wait()
+
+    def drain(source, kind):
+        all_but_one = source.at[pl.ds(0, n - 1)]
+        pltpu.make_async_copy(all_but_one, all_but_one, side_send.at[kind]).wait()
+
+    def send_inv(step, carry):
+        pltpu.make_async_remote_copy(
+            src_ref=isend.at[0], dst_ref=irecv.at[me],
+            send_sem=side_send.at[1], recv_sem=side_recv.at[1],
+            device_id=other(step), device_id_type=MESH,
+        ).start()
+        return carry
+
+    def forward(index, part, target_hi, target_lo):
+        here = pay.at[index, :, lanes[part]]
+        pltpu.make_async_remote_copy(
+            src_ref=here, dst_ref=here,
+            send_sem=send_sem.at[part], recv_sem=recv_sem.at[part, index],
+            device_id=(target_hi, target_lo), device_id_type=MESH,
+        ).start()
+
+    def arrive(index, part):
+        here = pay.at[index, :, lanes[part]]
+        pltpu.make_async_copy(here, here, recv_sem.at[part, index]).wait()
+
+    x_lo = lo + 1 - 2 * x
+    y_hi = hi + CORES - 2 * CORES * y
+    c_hi = hi + 1 - 2 * core
+
+    def turned_z(step):
+        return lax.rem(z + step, depth) * XDIM
+
+    def send_own(part):
+        forward(me, part, hi, x_lo)
+        forward(me, part, y_hi, lo)
+        for step in range(1, depth):
+            forward(me, part, hi, turned_z(step) + x)
+        forward(me, part, c_hi, lo)
+
+    def by_x(part, step):
+        return (part == 0) if part != 1 else (step % 2 == 0)
+
+    def relay(part):
+        for step in range(depth):
+            own_column = hi * n_lo + turned_z(step) + x
+            if step > 0:
+                arrive(own_column, part)
+                forward(own_column, part, hi, x_lo)
+                forward(own_column, part, y_hi, lo)
+                forward(own_column, part, c_hi, lo)
+            beside_x = hi * n_lo + turned_z(step) + 1 - x
+            arrive(beside_x, part)
+            if by_x(part, step):
+                forward(beside_x, part, y_hi, lo)
+            forward(beside_x, part, c_hi, lo)
+            beside_y = y_hi * n_lo + turned_z(step) + x
+            arrive(beside_y, part)
+            if not by_x(part, step):
+                forward(beside_y, part, hi, x_lo)
+            forward(beside_y, part, c_hi, lo)
+        for step in range(depth):
+            corner = y_hi * n_lo + turned_z(step) + 1 - x
+            arrive(corner, part)
+            forward(corner, part, c_hi, lo)
+
+    def from_core(part):
+        for own_y in (True, False):
+            base = (c_hi if own_y else lax.rem(c_hi + CORES, n_hi)) * n_lo
+            for block in range(n_lo):
+                arrive(base + block, part)
+
+    exchange(xsend, xrecv, 0)
+    lax.fori_loop(1, n, send_inv, 0)
+    irecv[me] = isend[0]
+    for part in range(3):
+        send_own(part)
+    relay(0)
+    from_core(0)
+    settle(xrecv, 0)
+    settle(irecv, 1)
+
+    for pair in range(n // 2):
+        at = slice(pair * 2 * rows, (pair + 1) * 2 * rows)
+        one, two = xrecv[2 * pair], xrecv[2 * pair + 1]
+        resid[0:half, at] = jnp.concatenate([one[:, :rows], two[:, :rows]], axis=1)
+        resid[half:mine, at] = jnp.concatenate([one[:, rows:], two[:, rows:]], axis=1)
+        low = lax.broadcasted_iota(jnp.int32, (1, 2 * rows), 1) < rows
+        inv_row[:, at] = jnp.where(low, irecv[2 * pair], irecv[2 * pair + 1])
+
+    group = n // 4
+    span = group * rows
+
+    def precondition():
+        def down(q, carry):
+            part = halves(resid[:, pl.ds(pl.multiple_of(q * span, span), span)], 0)
+            for j in range(group):
+                both = nn(part[:, j * rows : (j + 1) * rows], pay[q * group + j, :, 0:used])
+                coef[q * group + j] = both[:mine] + both[mine:]
+            return carry
+
+        lax.fori_loop(0, n // group, down, 0)
+        low = lax.broadcasted_iota(jnp.int32, (mine, 2 * rank), 1) < rank
+        for chunk in range(used // (2 * rank)):
+            at = slice(chunk * 2 * rank, (chunk + 1) * 2 * rank)
+            first, second = 2 * chunk, 2 * chunk + 1
+            if second == bits:
+                total = coef[0, :, at]
+                for k in range(1, n):
+                    total = total + coef[k, :, at]
+            for k in range(n):
+                own = coef[k, :, at]
+                left = own + coef[k ^ (1 << first), :, at]
+                right = total if second == bits else own + coef[k ^ (1 << second), :, at]
+                summed[k, :, at] = halves(jnp.where(low, left, right), 0)
+        both = nn(summed[...].reshape(n * 2 * mine, used), couple[0]).reshape(n, 2 * mine, used)
+        rest = nn(summed[:, :mine].reshape(n * mine, used), couple[1]).reshape(n, mine, used)
+        lifted[...] = halves(both[:, :mine] + both[:, mine:] + rest, 1)
+
+        def up(q, carry):
+            pieces = []
+            for j in range(group):
+                both = nt(lifted[q * group + j], pay[q * group + j, :, 0:used])
+                pieces.append(both[:mine] + both[mine:])
+            at = pl.ds(pl.multiple_of(q * span, span), span)
+            scaled[:, at] = inv_row[:, at] * resid[:, at] + jnp.concatenate(pieces, axis=1)
+            return carry
+
+        lax.fori_loop(0, n // group, up, 0)
+        return jnp.sum(resid[...] * scaled[...], axis=1, keepdims=True)
+
+    def apply_grm():
+        cut = [direct[:, h * width : (h + 1) * width].astype(bf16) for h in range(n_hi)]
+        total = [jnp.zeros((mine, width), f32) for _ in range(n_hi)]
+        for h in range(n_hi):
+            near, far = (h + 1) % n_hi, (h + 2) % n_hi
+            base = h * n_lo
+            full = pay[base : base + n_lo, :, lanes[1]].reshape(width, width)
+            total[h] = total[h] + nn(cut[h], full)
+            full = pay[base : base + n_lo, :, lanes[2]].reshape(width, width)
+            total[h] = total[h] + nn(cut[near], full)
+            total[near] = total[near] + nt(cut[h], full)
+            sums = {}
+            for r in range(2):
+                q = r if h < CORES else 1 - r
+                blocks = pay[
+                    base + r * (n_lo // 2) : base + (r + 1) * (n_lo // 2), :, used : used + quad
+                ].reshape(quad, quad)
+                sums["h", q] = nn(cut[far][:, r * quad : (r + 1) * quad], blocks)
+                sums["far", r] = nt(cut[h][:, q * quad : (q + 1) * quad], blocks)
+            total[h] = total[h] + jnp.concatenate([sums["h", 0], sums["h", 1]], axis=1)
+            total[far] = total[far] + jnp.concatenate([sums["far", 0], sums["far", 1]], axis=1)
+        for h in range(n_hi):
+            at = slice(h * width, (h + 1) * width)
+            image[:, at] = var_ref[0] * total[h] + var_ref[1] * direct[:, at]
+
+    energy = precondition()
+    direct[...] = scaled[...]
+    iterate[...] = jnp.zeros_like(iterate)
+    for part in (1, 2):
+        relay(part)
+        from_core(part)
+    for step in range(ITERS):
+        apply_grm()
+        curvature = jnp.sum(direct[...] * image[...], axis=1, keepdims=True)
+        alpha = jnp.where(steps_wanted > step, energy / curvature, 0.0)
+        iterate[...] = iterate[...] + alpha * direct[...]
+        resid[...] = resid[...] - alpha * image[...]
+        if step + 1 < ITERS:
+            fresh = precondition()
+            direct[...] = scaled[...] + (fresh / energy) * direct[...]
+            energy = fresh
+
+    for which, field in ((0, iterate), (1, resid)):
+        for pair in range(n // 2):
+            both = field[:, pair * 2 * rows : (pair + 1) * 2 * rows]
+            top, bottom = both[:half], both[half:]
+            osend[2 * pair, which] = jnp.concatenate([top[:, :rows], bottom[:, :rows]], axis=1)
+            osend[2 * pair + 1, which] = jnp.concatenate([top[:, rows:], bottom[:, rows:]], axis=1)
+    exchange(osend, orecv, 2)
+    for part in range(3):
+        sent = pay.at[pl.ds(0, n - 1), :, lanes[part]]
+        pltpu.make_async_copy(sent, sent, send_sem.at[part]).wait()
+    drain(xsend, 0)
+    drain(irecv, 1)
+    settle(orecv, 2)
+    for which, out_ref in ((0, sol_ref), (1, res_ref)):
+        got = orecv[:, which]
+        apart = jnp.concatenate([got[:, :, :rows], got[:, :, rows:]], axis=1)
+        out_ref[...] = apart.reshape(columns, rows).T
+    drain(osend, 2)
+
+
+def run_whole(mesh, grm, right_sides, inv_diag, bases, couplings, level_map, variance, iters):
+    n_hi, n_lo = mesh.shape["hi"], mesh.shape["lo"]
+    n = n_hi * n_lo
+    rows, columns = right_sides.shape
+    mine = columns // n
+    rank = couplings.shape[1]
+    used = n.bit_length() * rank
+    width = grm.shape[4]
+    samples = rows * n
+    f32, bf16 = jnp.float32, jnp.bfloat16
+    vmem = pl.BlockSpec(memory_space=pltpu.VMEM)
+    smem = pl.BlockSpec(memory_space=pltpu.SMEM)
+    field = pltpu.VMEM((mine, samples), f32)
+    tile = (mine // 2, 2 * rows)
+    return pl.pallas_call(
+        functools.partial(whole_kernel, n_hi, n_lo),
+        out_shape=(jax.ShapeDtypeStruct((rows, columns), f32),) * 2,
+        in_specs=[smem, smem] + [vmem] * 6,
+        out_specs=(vmem, vmem),
+        scratch_shapes=[
+            pltpu.VMEM((n, rows, used + width // 2 + 2 * width), bf16),
+            pltpu.VMEM((n,) + tile, f32),
+            pltpu.VMEM((n,) + tile, f32),
+            pltpu.VMEM((1, 1, 2 * rows), f32),
+            pltpu.VMEM((n, 1, 2 * rows), f32),
+            pltpu.VMEM((n, 2) + tile, f32),
+            pltpu.VMEM((n, 2) + tile, f32),
+            field, field, field, field, field,
+            pltpu.VMEM((1, samples), f32),
+            pltpu.VMEM((n, mine, used), f32),
+            pltpu.VMEM((n, 2 * mine, used), bf16),
+            pltpu.VMEM((n, 2 * mine, used), bf16),
+            pltpu.VMEM((2, used, used), bf16),
+            pltpu.SemaphoreType.DMA((3,)),
+            pltpu.SemaphoreType.DMA((3, n)),
+            pltpu.SemaphoreType.DMA((3,)),
+            pltpu.SemaphoreType.DMA((3,)),
+        ],
+        compiler_params=pltpu.CompilerParams(
+            collective_id=0, has_side_effects=True, vmem_limit_bytes=56 * 2**20
+        ),
+    )(
+        variance, level_map,
+        grm.reshape(grm.shape[0], rows, width), right_sides, inv_diag.reshape(1, rows),
+        bases, couplings, iters.reshape(1, columns),
+    )
+
+
 def solution(mesh):
     in_specs = (
         P(None, "lo", None, "hi", None),
@@ -108,4 +491,13 @@
         P(),
     )
     out_specs = (P(("hi", "lo"), None), P(("hi", "lo"), None))
-    return jax.shard_map(local, mesh=mesh, in_specs=in_specs, out_specs=out_specs, check_vma=False)
+
+    def program(*arrays):
+        body = local
+        if fits_one_device(mesh, arrays[0], arrays[1], arrays[3], arrays[4]):
+            body = functools.partial(run_whole, mesh)
+        return jax.shard_map(
+            body, mesh=mesh, in_specs=in_specs, out_specs=out_specs, check_vma=False
+        )(*arrays)
+
+    return program

time: 808 us -> 102 us (0.13)
  waiting for transfers between devices: 411 us -> 0 us
  blocking collectives: 291 us -> 0 us
  Pallas kernels: 0 us -> 98.9 us
  matrix products: 43.6 us -> 0 us
  starting transfers between devices: 23 us -> 0 us
  other arithmetic: 18.3 us -> 0 us
  between operations: 14.7 us -> 0.65 us
    psum x3 -> x0, waiting for transfers between devices: 346 us -> none  [precondition(): lax.psum((coefficients[level_total - 1], partial_energy), ('hi', 'lo'))]
    psum x5 -> x0, blocking collectives: 197 us -> none  [the longest x3 118 us: precondition(): lax.psum((coefficients[level_total - 1], partial_energy), ('hi', 'lo'))]
    pallas_call x0 -> x1, Pallas kernels: none -> 98.9 us  [run_whole(): pl.pallas_call(functools.partial(whole_kernel, n_hi, n_lo), out_shape=(ja...]
    all_gather x3 -> x0, blocking collectives: 93.7 us -> none  [local(): lax.all_gather(rounded, 'lo', axis=0, tiled=True)]
    reduce_scatter x3 -> x0, waiting for transfers between devices: 64.5 us -> none  [local(): lax.psum_scatter(partial_value, 'hi', scatter_dimension=0, tiled=True)]
    dot_general x50 -> x0, matrix products: 43.6 us -> none  [the longest x15 20.4 us: level_pieces(): own_part = jnp.einsum('l,lrb->rb', select, coefficients)]
    ppermute x15 -> x0, starting transfers between devices: 22.8 us -> none  [from_partner(): return lax.ppermute(value, axis, pairs)]
  transfers between devices with their start and end apart: 21 -> 0, of which waited for: 6 -> 0; matrix products, arithmetic and copies ran while one was open for 3% -> 0% of each run, Pallas kernels for 0% -> 0%
where the time goes in v1:
time: 102 us
  Pallas kernels  98.9 us (97%)
  local copies, waits for them, and re-layouts  2.26 us (2%)
    pallas_call x1, Pallas kernels, run_whole(): pl.pallas_call(functools.partial(whole_kernel, n_hi, n_lo), out_shape=(ja...  98.9 us
    unnamed x4, local copies, waits for them, and re-layouts  2.26 us

profile of v1, /device:TPU:0, one launch (start us, length us, event | category | flops | bytes accessed | tf_op | source)
XLA Modules:
  0.0 101.8 jit_solution(9117992839130221340)
XLA Ops:
  0.6 98.9 %shard_map.95 = (f32[64,512]{1,0:T(8,128)}, f32[64,512]{1,0:T(8,128)}) custom-call(f32[2]{0:T(128)} %var_ref.1, s32[8]{0:T(128)} %level_ref.1, bf16[4,64,512]{2,1,0:T(8,128)(2,1)} %bitcast.3, f32[64,512]{1,0:T(8,128)} %rhs_ref.1, f32[1,64]{1,0:T(1,128)} %bitcast.5, f32[64,576]{1,0:T(8,128)} %bases_ref.1, f32[9,64,64]{2,1,0:T(8,128)} %coup_ref.1, ...), custom_call_target="tpu_custom_call" | custom-call | tf_op jit(solution)/shard_map/pallas_call | solution.py:448
  99.5 0.0 copy-start
  99.5 1.6 %copy.12 = f32[64,512]{1,0:T(8,128)} copy(f32[64,512]{1,0:T(8,128)} %get-tuple-element.4) | data formatting | bytes 262144
  101.1 0.0 copy-done
  101.1 0.7 copy.13
Async XLA Ops:
  99.5 1.6 %copy-start = (f32[64,512]{1,0:T(8,128)S(1)}, f32[64,512]{1,0:T(8,128)}, u32[]{:S(2)}) copy-start(f32[64,512]{1,0:T(8,128)} %get-tuple-element.5) | copy-start | bytes 393220

commit v2 on v1

--- a/solution.py
+++ b/solution.py
@@ -125,6 +125,7 @@
 
 CORES = 2
 XDIM = 2
+LAG = 4
 
 
 def nt(a, b):
@@ -146,7 +147,7 @@
     var_ref, level_ref,
     grm_ref, rhs_ref, inv_ref, bases_ref, coup_ref, iters_ref,
     sol_ref, res_ref,
-    pay, xsend, xrecv, isend, irecv, osend, orecv,
+    pay, near_pay, next_pay, xsend, xrecv, isend, irecv, osend, orecv,
     resid, direct, image, iterate, scaled, inv_row,
     coef, summed, lifted, couple,
     send_sem, recv_sem, side_send, side_recv,
@@ -188,11 +189,7 @@
     wanted = wanted + column_id % rank
     pick = lax.broadcasted_iota(jnp.int32, (levels * rank, used), 0) == wanted
     own_bases = nn(bases_ref[...].astype(bf16), pick.astype(f32).astype(bf16))
-    lanes = (
-        slice(0, used + quad),
-        slice(used + quad, used + quad + width),
-        slice(used + quad + width, used + quad + 2 * width),
-    )
+    parts = (pay, near_pay, next_pay)
     pay[me, :, 0:used] = own_bases.astype(bf16)
     across = lax.rem(hi + CORES, n_hi)
     upper = jnp.where(hi < CORES, lo >= n_lo // 2, lo < n_lo // 2)
@@ -200,8 +197,8 @@
     pay[me, :, used : used + quad] = jnp.where(
         upper, both[:, quad:].astype(f32), both[:, :quad].astype(f32)
     ).astype(bf16)
-    pay[me, :, lanes[1]] = grm_ref[hi]
-    pay[me, :, lanes[2]] = grm_ref[lax.rem(hi + 1, n_hi)]
+    near_pay[me] = grm_ref[hi]
+    next_pay[me] = grm_ref[lax.rem(hi + 1, n_hi)]
 
     turned = rhs_ref[...].T.reshape(n, mine, rows)
     xsend[...] = jnp.concatenate([turned[:, :half], turned[:, half:]], axis=2)
@@ -253,7 +250,7 @@
         return carry
 
     def forward(index, part, target_hi, target_lo):
-        here = pay.at[index, :, lanes[part]]
+        here = parts[part].at[index]
         pltpu.make_async_remote_copy(
             src_ref=here, dst_ref=here,
             send_sem=send_sem.at[part], recv_sem=recv_sem.at[part, index],
@@ -261,7 +258,7 @@
         ).start()
 
     def arrive(index, part):
-        here = pay.at[index, :, lanes[part]]
+        here = parts[part].at[index]
         pltpu.make_async_copy(here, here, recv_sem.at[part, index]).wait()
 
     x_lo = lo + 1 - 2 * x
@@ -278,31 +275,39 @@
             forward(me, part, hi, turned_z(step) + x)
         forward(me, part, c_hi, lo)
 
-    def by_x(part, step):
-        return (part == 0) if part != 1 else (step % 2 == 0)
-
-    def relay(part):
-        for step in range(depth):
-            own_column = hi * n_lo + turned_z(step) + x
-            if step > 0:
-                arrive(own_column, part)
-                forward(own_column, part, hi, x_lo)
-                forward(own_column, part, y_hi, lo)
-                forward(own_column, part, c_hi, lo)
-            beside_x = hi * n_lo + turned_z(step) + 1 - x
-            arrive(beside_x, part)
-            if by_x(part, step):
-                forward(beside_x, part, y_hi, lo)
-            forward(beside_x, part, c_hi, lo)
-            beside_y = y_hi * n_lo + turned_z(step) + x
-            arrive(beside_y, part)
-            if not by_x(part, step):
-                forward(beside_y, part, hi, x_lo)
-            forward(beside_y, part, c_hi, lo)
-        for step in range(depth):
-            corner = y_hi * n_lo + turned_z(step) + 1 - x
-            arrive(corner, part)
-            forward(corner, part, c_hi, lo)
+    def column(part, step):
+        if step == 0:
+            return
+        index = hi * n_lo + turned_z(step) + x
+        arrive(index, part)
+        forward(index, part, hi, x_lo)
+        forward(index, part, y_hi, lo)
+        forward(index, part, c_hi, lo)
+
+    def beside(part, step):
+        index = hi * n_lo + turned_z(step) + 1 - x
+        arrive(index, part)
+        if step % 2 == 0:
+            forward(index, part, y_hi, lo)
+        forward(index, part, c_hi, lo)
+        index = y_hi * n_lo + turned_z(step) + x
+        arrive(index, part)
+        if step % 2 == 1:
+            forward(index, part, hi, x_lo)
+        forward(index, part, c_hi, lo)
+
+    def corner(part, step):
+        index = y_hi * n_lo + turned_z(step) + 1 - x
+        arrive(index, part)
+        forward(index, part, c_hi, lo)
+
+    def relay(first, last):
+        for t in range(first, last):
+            for move, late in ((column, 0), (beside, LAG), (corner, 2 * LAG)):
+                if 0 <= t - late < 3 * depth:
+                    move((t - late) // depth, (t - late) % depth)
+            if t == depth - 1:
+                send_own(2)
 
     def from_core(part):
         for own_y in (True, False):
@@ -313,9 +318,10 @@
     exchange(xsend, xrecv, 0)
     lax.fori_loop(1, n, send_inv, 0)
     irecv[me] = isend[0]
-    for part in range(3):
-        send_own(part)
-    relay(0)
+    send_own(0)
+    send_own(1)
+    ready = depth + 2 * LAG
+    relay(0, ready)
     from_core(0)
     settle(xrecv, 0)
     settle(irecv, 1)
@@ -375,9 +381,9 @@
         for h in range(n_hi):
             near, far = (h + 1) % n_hi, (h + 2) % n_hi
             base = h * n_lo
-            full = pay[base : base + n_lo, :, lanes[1]].reshape(width, width)
+            full = near_pay[base : base + n_lo].reshape(width, width)
             total[h] = total[h] + nn(cut[h], full)
-            full = pay[base : base + n_lo, :, lanes[2]].reshape(width, width)
+            full = next_pay[base : base + n_lo].reshape(width, width)
             total[h] = total[h] + nn(cut[near], full)
             total[near] = total[near] + nt(cut[h], full)
             sums = {}
@@ -397,9 +403,9 @@
     energy = precondition()
     direct[...] = scaled[...]
     iterate[...] = jnp.zeros_like(iterate)
-    for part in (1, 2):
-        relay(part)
-        from_core(part)
+    relay(ready, 3 * depth + 2 * LAG)
+    from_core(1)
+    from_core(2)
     for step in range(ITERS):
         apply_grm()
         curvature = jnp.sum(direct[...] * image[...], axis=1, keepdims=True)
@@ -419,7 +425,7 @@
             osend[2 * pair + 1, which] = jnp.concatenate([top[:, rows:], bottom[:, rows:]], axis=1)
     exchange(osend, orecv, 2)
     for part in range(3):
-        sent = pay.at[pl.ds(0, n - 1), :, lanes[part]]
+        sent = parts[part].at[pl.ds(0, n - 1)]
         pltpu.make_async_copy(sent, sent, send_sem.at[part]).wait()
     drain(xsend, 0)
     drain(irecv, 1)
@@ -451,7 +457,9 @@
         in_specs=[smem, smem] + [vmem] * 6,
         out_specs=(vmem, vmem),
         scratch_shapes=[
-            pltpu.VMEM((n, rows, used + width // 2 + 2 * width), bf16),
+            pltpu.VMEM((n, rows, used + width // 2), bf16),
+            pltpu.VMEM((n, rows, width), bf16),
+            pltpu.VMEM((n, rows, width), bf16),
             pltpu.VMEM((n,) + tile, f32),
             pltpu.VMEM((n,) + tile, f32),
             pltpu.VMEM((1, 1, 2 * rows), f32),

time: 102 us -> 72 us (0.71)
  Pallas kernels: 98.9 us -> 68.9 us
    pallas_call x1, Pallas kernels: 98.9 us -> 68.9 us  [run_whole(): pl.pallas_call(functools.partial(whole_kernel, n_hi, n_lo), out_shape=(ja...]
where the time goes in v2:
time: 72 us; the launch traced here: 71.9 us
  Pallas kernels  68.9 us (96%)
  local copies, waits for them, and re-layouts  2.26 us (3%)
    pallas_call x1, Pallas kernels, run_whole(): pl.pallas_call(functools.partial(whole_kernel, n_hi, n_lo), out_shape=(ja...  68.9 us
    unnamed x4, local copies, waits for them, and re-layouts  2.26 us

profile of v2, /device:TPU:0, one launch (start us, length us, event | category | flops | bytes accessed | tf_op | source)
XLA Modules:
  0.0 71.9 jit_solution(1744616716960970285)
XLA Ops:
  0.6 68.9 %shard_map.95 = (f32[64,512]{1,0:T(8,128)}, f32[64,512]{1,0:T(8,128)}) custom-call(f32[2]{0:T(128)} %var_ref.1, s32[8]{0:T(128)} %level_ref.1, bf16[4,64,512]{2,1,0:T(8,128)(2,1)} %bitcast.3, f32[64,512]{1,0:T(8,128)} %rhs_ref.1, f32[1,64]{1,0:T(1,128)} %bitcast.5, f32[64,576]{1,0:T(8,128)} %bases_ref.1, f32[9,64,64]{2,1,0:T(8,128)} %coup_ref.1, ...), custom_call_target="tpu_custom_call" | custom-call | tf_op jit(solution)/shard_map/pallas_call | solution.py:454
  69.6 0.0 copy-start
  69.6 1.6 %copy.12 = f32[64,512]{1,0:T(8,128)} copy(f32[64,512]{1,0:T(8,128)} %get-tuple-element.4) | data formatting | bytes 262144
  71.2 0.0 copy-done
  71.2 0.7 copy.13
Async XLA Ops:
  69.6 1.6 %copy-start = (f32[64,512]{1,0:T(8,128)S(1)}, f32[64,512]{1,0:T(8,128)}, u32[]{:S(2)}) copy-start(f32[64,512]{1,0:T(8,128)} %get-tuple-element.5) | copy-start | bytes 393220

commit v3 on v2

--- a/solution.py
+++ b/solution.py
@@ -233,6 +233,19 @@
         lax.fori_loop(1, n, send, 0)
         target[me] = source[me]
 
+    def exchange_field(which):
+        def send(step, carry):
+            peer = lax.rem(me + step, n)
+            pltpu.make_async_remote_copy(
+                src_ref=osend.at[peer, which], dst_ref=orecv.at[me, which],
+                send_sem=side_send.at[2 + which], recv_sem=side_recv.at[2 + which],
+                device_id=(peer // n_lo, lax.rem(peer, n_lo)), device_id_type=MESH,
+            ).start()
+            return carry
+
+        lax.fori_loop(1, n, send, 0)
+        orecv[me, which] = osend[me, which]
+
     def settle(target, kind):
         all_but_one = target.at[pl.ds(0, n - 1)]
         pltpu.make_async_copy(all_but_one, all_but_one, side_recv.at[kind]).wait()
@@ -315,10 +328,10 @@
             for block in range(n_lo):
                 arrive(base + block, part)
 
+    send_own(0)
     exchange(xsend, xrecv, 0)
     lax.fori_loop(1, n, send_inv, 0)
     irecv[me] = isend[0]
-    send_own(0)
     send_own(1)
     ready = depth + 2 * LAG
     relay(0, ready)
@@ -423,18 +436,19 @@
             top, bottom = both[:half], both[half:]
             osend[2 * pair, which] = jnp.concatenate([top[:, :rows], bottom[:, :rows]], axis=1)
             osend[2 * pair + 1, which] = jnp.concatenate([top[:, rows:], bottom[:, rows:]], axis=1)
-    exchange(osend, orecv, 2)
+        exchange_field(which)
     for part in range(3):
         sent = parts[part].at[pl.ds(0, n - 1)]
         pltpu.make_async_copy(sent, sent, send_sem.at[part]).wait()
     drain(xsend, 0)
     drain(irecv, 1)
-    settle(orecv, 2)
     for which, out_ref in ((0, sol_ref), (1, res_ref)):
+        settle(orecv.at[:, which], 2 + which)
         got = orecv[:, which]
         apart = jnp.concatenate([got[:, :, :rows], got[:, :, rows:]], axis=1)
         out_ref[...] = apart.reshape(columns, rows).T
-    drain(osend, 2)
+    for which in range(2):
+        drain(osend.at[:, which], 2 + which)
 
 
 def run_whole(mesh, grm, right_sides, inv_diag, bases, couplings, level_map, variance, iters):
@@ -474,8 +488,8 @@
             pltpu.VMEM((2, used, used), bf16),
             pltpu.SemaphoreType.DMA((3,)),
             pltpu.SemaphoreType.DMA((3, n)),
-            pltpu.SemaphoreType.DMA((3,)),
-            pltpu.SemaphoreType.DMA((3,)),
+            pltpu.SemaphoreType.DMA((4,)),
+            pltpu.SemaphoreType.DMA((4,)),
         ],
         compiler_params=pltpu.CompilerParams(
             collective_id=0, has_side_effects=True, vmem_limit_bytes=56 * 2**20

time: 72 us -> 71 us (0.986)
  Pallas kernels: 68.9 us -> 68 us
    pallas_call x1, Pallas kernels: 68.9 us -> 68 us  [run_whole(): pl.pallas_call(functools.partial(whole_kernel, n_hi, n_lo), out_shape=(ja...]
where the time goes in v3:
time: 71 us; the launch traced here: 70.9 us
  Pallas kernels  68 us (96%)
  local copies, waits for them, and re-layouts  2.26 us (3%)
    pallas_call x1, Pallas kernels, run_whole(): pl.pallas_call(functools.partial(whole_kernel, n_hi, n_lo), out_shape=(ja...  68 us
    unnamed x4, local copies, waits for them, and re-layouts  2.26 us

profile of v3, /device:TPU:0, one launch (start us, length us, event | category | flops | bytes accessed | tf_op | source)
XLA Modules:
  0.0 70.9 jit_solution(12385883001924133214)
XLA Ops:
  0.6 68.0 %shard_map.95 = (f32[64,512]{1,0:T(8,128)}, f32[64,512]{1,0:T(8,128)}) custom-call(f32[2]{0:T(128)} %var_ref.1, s32[8]{0:T(128)} %level_ref.1, bf16[4,64,512]{2,1,0:T(8,128)(2,1)} %bitcast.3, f32[64,512]{1,0:T(8,128)} %rhs_ref.1, f32[1,64]{1,0:T(1,128)} %bitcast.5, f32[64,576]{1,0:T(8,128)} %bases_ref.1, f32[9,64,64]{2,1,0:T(8,128)} %coup_ref.1, ...), custom_call_target="tpu_custom_call" | custom-call | tf_op jit(solution)/shard_map/pallas_call | solution.py:468
  68.6 0.0 copy-start
  68.6 1.6 %copy.12 = f32[64,512]{1,0:T(8,128)} copy(f32[64,512]{1,0:T(8,128)} %get-tuple-element.4) | data formatting | bytes 262144
  70.2 0.0 copy-done
  70.2 0.7 copy.13
Async XLA Ops:
  68.6 1.6 %copy-start = (f32[64,512]{1,0:T(8,128)S(1)}, f32[64,512]{1,0:T(8,128)}, u32[]{:S(2)}) copy-start(f32[64,512]{1,0:T(8,128)} %get-tuple-element.5) | copy-start | bytes 393220
